TPU v7x, 8 devices: a whole 2x2x1 slice. The times are simulated.
8 devices in a mesh: dp: 2 (over y, z), tp: 4 (over x, core).
Axes of the slice: x: 2, y: 2, z: 1, core: 2. Of those that a mesh axis runs over, the one named last changes fastest.
Arguments:
- x: bfloat16 [128, 2560], P('dp'), parts along dimension 0
- k_cache: bfloat16 [128, 2048, 8, 128], P('dp', None, 'tp'), parts along dimension 0
- v_cache: bfloat16 [128, 2048, 8, 128], P('dp', None, 'tp'), parts along dimension 0
- gain_a: bfloat16 [2560], replicated
- wq: bfloat16 [2560, 4096], P(None, 'tp')
- wo: bfloat16 [4096, 2560], P('tp')
- gain_m: bfloat16 [2560], replicated
- w_gate: bfloat16 [2560, 9728], P(None, 'tp')
- w_up: bfloat16 [2560, 9728], P(None, 'tp')
- w_down: bfloat16 [9728, 2560], P('tp')
Outputs:
- output: bfloat16 [128, 2560], P('dp'), parts along dimension 0
There are 2 independent parts. A program takes and returns all parts, laid end to end along the dimension named above; an argument that names none is the same for every part.
All inputs are finite; a program needn't handle non-finite values.
Results may differ from a plain program's by a relative error of at most 0.017.
Values are sent between devices in bfloat16 or wider.
A program may use at most 2 GiB of HBM per device.

v0:
```python
import jax
import jax.numpy as jnp
from jax import lax
from jax.sharding import PartitionSpec as P

HEAD = 128
THETA = 10000


def normed(x, gain):
    wide = x.astype(jnp.float32)
    scale = lax.rsqrt(jnp.mean(wide * wide, -1, keepdims=True) + 1e-6)
    return (wide * scale * gain.astype(jnp.float32)).astype(jnp.bfloat16)


def turned(t, place, theta):
    half = t.shape[-1] // 2
    angle = place.astype(jnp.float32)[:, None] * theta ** (-jnp.arange(half, dtype=jnp.float32) / half)
    cos, sin = jnp.cos(angle)[:, None], jnp.sin(angle)[:, None]
    a, b = t[..., :half].astype(jnp.float32), t[..., half:].astype(jnp.float32)
    return jnp.concatenate([a * cos - b * sin, b * cos + a * sin], -1).astype(jnp.bfloat16)


def matmul(a, w):
    return jnp.dot(a, w, preferred_element_type=jnp.float32).astype(jnp.bfloat16)


def einsum(form, a, b):
    return jnp.einsum(form, a.astype(jnp.float32), b.astype(jnp.float32))


def seen_by(a, wq, k_cache, v_cache, head, theta):
    batch, cache, kv_heads = k_cache.shape[:3]
    place = jnp.full((batch,), cache - 1)
    q = turned(matmul(a, wq).reshape(batch, -1, head), place, theta).reshape(batch, kv_heads, -1, head)
    scores = einsum("bgsd,bugd->bgsu", q, k_cache) * head**-0.5
    weights = jax.nn.softmax(scores, -1).astype(jnp.bfloat16)
    return einsum("bgsu,bugd->bgsd", weights, v_cache).astype(jnp.bfloat16).reshape(batch, -1)


def hidden_of(b, w_gate, w_up):
    gate = jnp.dot(b, w_gate, preferred_element_type=jnp.float32)
    up = jnp.dot(b, w_up, preferred_element_type=jnp.float32)
    return (jax.nn.silu(gate) * up).astype(jnp.bfloat16)


def solution(mesh):
    def added(t, term):
        return (t.astype(jnp.float32) + lax.psum(term.astype(jnp.bfloat16), "tp").astype(jnp.float32)).astype(jnp.bfloat16)

    def step(x, k_cache, v_cache, gain_a, wq, wo, gain_m, w_gate, w_up, w_down):
        seen = seen_by(normed(x, gain_a), wq, k_cache, v_cache, HEAD, THETA)
        h = added(x, jnp.dot(seen, wo, preferred_element_type=jnp.float32))
        return added(h, jnp.dot(hidden_of(normed(h, gain_m), w_gate, w_up), w_down, preferred_element_type=jnp.float32))

    states, cache, columns, rows_of = P("dp", None), P("dp", None, "tp", None), P(None, "tp"), P("tp", None)
    return jax.shard_map(
        step,
        mesh=mesh,
        in_specs=(states, cache, cache, P(None), columns, rows_of, P(None), columns, columns, rows_of),
        out_specs=states,
        check_vma=False,
    )
```

profile of v0, /device:TPU:0, one launch (start us, length us, event | category | flops | bytes accessed | tf_op | source)
XLA Modules:
  0.0 165.5 jit_solution(2410825452117172100)
XLA Ops:
  6.5 0.0 all-reduce.3.cloned.1.call-start
  6.6 0.7 convert_element_type.63
  7.3 1.1 fusion.13
  8.4 3.7 %fusion.12 = bf16[8,8,8,128]{3,1,2,0:T(8,128)(2,1)S(1)} fusion(bf16[2560,1024]{1,0:T(8,128)(2,1)} %param.14, bf16[64,2560]{1,0:T(8,128)(2,1)} %param.10, f32[2560]{0:T(1024)S(1)} %convert_element_type.63, f32[64]{0:T(128)S(1)} %add_rsqrt_fusion.1), kind=kOutput, calls=%fused_computation.17 | convolution fusion | flops 336265216 | bytes 5712128 | tf_op jit(solution)/shard_map/dot_general | solution.py:25
  12.2 0.1 fusion.29
  12.3 35.4 %fusion.45 = (f32[64,2,4]{2,1,0:T(2,128)S(1)}, f32[64,2,4,2048]{3,2,1,0:T(4,128)}) fusion(bf16[64,2048,2,128]{3,2,1,0:T(2,128)(2,1)} %param.11, bf16[64,2,4,64]{3,2,1,0:T(4,128)(2,1)S(1)} %bitcast.13, bf16[64,2,4,64]{3,2,1,0:T(4,128)(2,1)S(1)} %bitcast.12), kind=kOutput, calls=%fused_computation.58 | convolution fusion | flops 271845376 | bytes 71436288 | tf_op jit(solution)/shard_map/sub | solution.py:37
  47.7 0.0 copy-start.1
  47.7 0.0 copy-start
  47.8 26.6 %fusion.9 = bf16[64,2,4,128]{3,2,1,0:T(4,128)(2,1)S(1)} fusion(bf16[64,2048,2,128]{3,2,1,0:T(2,128)(2,1)} %param.12, f32[64,2,4,2048]{3,2,1,0:T(4,128)} %get-tuple-element.10, f32[64,2,4]{2,1,0:T(2,128)S(1)} %get-tuple-element.9), kind=kOutput, calls=%fused_computation.15 | convolution fusion | flops 270598144 | bytes 71436288 | tf_op jit(solution)/shard_map/bgsu,bugd->bgsd/dot_general | solution.py:29
  74.3 0.1 reshape.40
  74.4 4.2 %convolution_convert_fusion = bf16[64,2560]{1,0:T(8,128)(2,1)} fusion(bf16[64,1024]{1,0:T(8,128)(2,1)S(1)} %reshape.40, bf16[1024,2560]{1,0:T(8,128)(2,1)} %param.15), kind=kOutput, calls=%fused_computation.11 | convolution fusion | flops 335708160 | bytes 5701632 | tf_op jit(solution)/shard_map/dot_general | solution.py:53
  78.6 0.0 all-reduce.3.cloned.1.call-update
  78.6 0.2 all-reduce.5.cloned.1.call-start
  78.9 0.0 copy-done.1
  78.9 29.6 %all-reduce.3.cloned.1.call-done = bf16[64,2560]{1,0:T(8,128)(2,1)} async-done(((bf16[64,2560]{1,0:T(8,128)(2,1)}), bf16[64,2560]{1,0:T(8,128)(2,1)}) %all-reduce.3.cloned.1.call-update) | async-done | bytes 327696 | tf_op jit(solution)/shard_map/psum | solution.py:49
  108.5 0.0 copy-done
  108.5 1.2 fusion.17
  109.7 6.9 %fusion.37 = f32[64,2432]{1,0:T(8,128)S(1)} fusion(bf16[2560,2432]{1,0:T(8,128)(2,1)} %param.17, bf16[64,2560]{1,0:T(8,128)(2,1)S(1)} %get-tuple-element.6, f32[2560]{0:T(1024)S(1)} %convert_element_type.74, f32[64]{0:T(128)S(1)} %add_rsqrt_fusion), kind=kOutput, calls=%fused_computation.49 | convolution fusion | flops 797573120 | bytes 13412608 | tf_op jit(solution)/shard_map/dot_general | solution.py:42
  116.6 13.3 %convolution_convert_fusion.1 = bf16[64,2560]{1,0:T(8,128)(2,1)} fusion(bf16[2432,2560]{1,0:T(8,128)(2,1)} %param.19, bf16[2560,2432]{1,0:T(8,128)(2,1)} %param.18, f32[64,2432]{1,0:T(8,128)S(1)} %fusion.37, bf16[64,2560]{1,0:T(8,128)(2,1)S(1)} %get-tuple-element.6, f32[2560]{0:T(1024)S(1)} %convert_element_type.74, f32[64]{0:T(128)S(1)} %add_rsqrt_fusion), kind=kOutput, calls=%fused_computation.12 | convolution fusion | flops 1595588608 | bytes 26192128 | tf_op jit(solution)/shard_map/dot_general | solution.py:54
  129.8 0.0 all-reduce.5.cloned.1.call-update
  129.9 27.0 %all-reduce.5.cloned.1.call-done = bf16[64,2560]{1,0:T(8,128)(2,1)} async-done(((bf16[64,2560]{1,0:T(8,128)(2,1)}), bf16[64,2560]{1,0:T(8,128)(2,1)}) %all-reduce.5.cloned.1.call-update) | async-done | bytes 327696 | tf_op jit(solution)/shard_map/psum | solution.py:49
  156.9 1.8 %fusion.20 = bf16[64,2560]{1,0:T(8,128)(2,1)} fusion(bf16[64,2560]{1,0:T(8,128)(2,1)S(1)} %get-tuple-element.6, bf16[64,2560]{1,0:T(8,128)(2,1)} %all-reduce.5.cloned.1.call-done), kind=kLoop, calls=%fused_computation.31 | loop fusion | flops 655360 | bytes 983040 | tf_op jit(solution)/shard_map/convert_element_type | solution.py:49
  (5 shorter events, 0.1 us)
Async XLA Ops:
  6.5 102.0 %all-reduce.3.cloned.1.call-start = ((), (), s32[]{:S(2)}) async-start(), calls=%async_computation | async-start | bytes 655360 | tf_op jit(solution)/shard_map/psum | solution.py:49
  47.7 31.2 %copy-start.1 = (bf16[2560]{0:T(1024)(128)(2,1)S(1)}, bf16[2560]{0:T(1024)(128)(2,1)}, u32[]{:S(2)}) copy-start(bf16[2560]{0:T(1024)(128)(2,1)} %param.16) | copy-start | bytes 15364
  47.7 60.8 %copy-start = (bf16[64,2560]{1,0:T(8,128)(2,1)S(1)}, bf16[64,2560]{1,0:T(8,128)(2,1)}, u32[]{:S(2)}) copy-start(bf16[64,2560]{1,0:T(8,128)(2,1)} %param.10) | copy-start | bytes 983044
  78.6 78.3 %all-reduce.5.cloned.1.call-start = ((), (), s32[]{:S(2)}) async-start(), calls=%async_computation.1 | async-start | bytes 655360 | tf_op jit(solution)/shard_map/psum | solution.py:49
Sparse Core Ops, SparseCore 0:
  78.8 29.6 all-reduce.2
  130.0 26.8 all-reduce.4
where the time goes:
time: 166 us
  matrix products  90 us (54%)
  waiting for transfers between devices  56.7 us (34%)
  between operations  13.5 us (8%)
  other arithmetic  5 us (3%)
    psum x2, waiting for transfers between devices, added(): lax.psum(term.astype(jnp.bfloat16), 'tp').astype(jnp.float32)  56.6 us
    sub x1, matrix products, seen_by(): weights = jax.nn.softmax(scores, -1).astype(jnp.bfloat16)  35.4 us
    dot_general x1, matrix products, einsum(): return jnp.einsum(form, a.astype(jnp.float32), b.astype(jnp.float32))  26.6 us
    dot_general x1, matrix products, step(): jnp.dot(hidden_of(normed(h, gain_m), w_gate, w_up), w_down, preferred_ele...  13.3 us
    dot_general x1, matrix products, hidden_of(): gate = jnp.dot(b, w_gate, preferred_element_type=jnp.float32)  6.87 us
    dot_general x1, matrix products, step(): h = added(x, jnp.dot(seen, wo, preferred_element_type=jnp.float32))  4.23 us
    dot_general x1, matrix products, matmul(): jnp.dot(a, w, preferred_element_type=jnp.float32).astype(jnp.bfloat16)  3.69 us
  transfers between devices with their start and end apart: 2, of which 2 were waited for; matrix products, arithmetic and copies ran while one was open for 0% of the time, Pallas kernels for 0%

commit v1 on v0

v1 whole, which is shorter than its diff:
```python
import functools
import math

import jax
import jax.numpy as jnp
import numpy as np
from jax import lax
from jax.experimental import pallas as pl
from jax.experimental.pallas import tpu as pltpu
from jax.sharding import PartitionSpec as P

THETA = 10000
MESH = pl.DeviceIdType.MESH
F32, BF16 = jnp.float32, jnp.bfloat16

GROUP = 2
SLOTS = 8


def widths_of(total, width):
    return [(at, min(width, total - at)) for at in range(0, total, width)]


def rotary(head, place):
    half = head // 2
    angle = place * float(THETA) ** (-np.arange(half, dtype=np.float64) / half)
    cos, sin = np.cos(angle), np.sin(angle)
    rows = np.stack([np.concatenate([cos, cos]), np.concatenate([-sin, sin])])
    return np.broadcast_to(rows[:, None], (2, 8, head)).astype(np.float32)


def normed(x, gain):
    scale = lax.rsqrt(jnp.mean(x * x, -1, keepdims=True) + 1e-6)
    return (x * scale * gain).astype(BF16)


def layer(dims, x_hbm, k_hbm, v_hbm, ga_hbm, wq_hbm, wo_hbm, gm_hbm, wg_hbm, wu_hbm, wd_hbm, rot_hbm, y_ref, *scratch):
    batch, d, heads, kv, head, rows, ff = dims
    qcols = heads * head
    half = batch // 2
    ffw, dw, qw = widths_of(ff, 512), widths_of(d, 512), widths_of(qcols, 512)
    it = iter(scratch)

    def take(n):
        return [next(it) for _ in range(n)]

    (kbuf, vbuf, xbuf, gab, gmb, rot, abuf, qbuf, sa, sb, seen, hbuf, bbuf, hidden, part) = take(15)
    wob = take(len(dw))
    gb, ub = take(len(ffw)), take(len(ffw))
    db = take(len(dw))
    sends1, recvs1, sends2, recvs2, final = take(5)
    (small_sem, wq_sem, k_sem, v_sem, wo_sem, g_sem, u_sem, d_sem, ss1, rs1, ss2, rs2, ss3, rs3) = take(14)

    tp = lax.axis_index("tp")
    core = lax.rem(tp, 2)
    chip = lax.div(tp, 2)
    partner = chip * 2 + 1 - core
    across = (1 - chip) * 2 + core

    barrier = pltpu.get_barrier_semaphore()
    for other in (partner, across):
        pl.semaphore_signal(barrier, inc=1, device_id={"tp": other}, device_id_type=MESH)

    copy = pltpu.make_async_copy
    smalls = [copy(x_hbm, xbuf, small_sem.at[0]), copy(ga_hbm, gab, small_sem.at[1]), copy(gm_hbm, gmb, small_sem.at[2]), copy(rot_hbm, rot, small_sem.at[3])]
    for c in smalls:
        c.start()
    wqs = [copy(wq_hbm.at[:, pl.ds(at, w)], gb[i].at[:, pl.ds(0, w)], wq_sem.at[i]) for i, (at, w) in enumerate(qw)]
    for c in wqs:
        c.start()

    def k_copy(seq, slot):
        return copy(k_hbm.at[seq], kbuf.at[slot], k_sem.at[slot])

    def v_copy(seq, slot):
        return copy(v_hbm.at[seq], vbuf.at[slot], v_sem.at[slot])

    for s in range(SLOTS):
        k_copy(s, s).start()
        v_copy(s, s).start()

    wos = [copy(wo_hbm.at[:, pl.ds(at, w)], wob[i], wo_sem.at[i]) for i, (at, w) in enumerate(dw)]
    gs = [copy(wg_hbm.at[:, pl.ds(at, w)], gb[i], g_sem.at[i]) for i, (at, w) in enumerate(ffw)]
    us = [copy(wu_hbm.at[:, pl.ds(at, w)], ub[i], u_sem.at[i]) for i, (at, w) in enumerate(ffw)]
    ds = [copy(wd_hbm.at[:, pl.ds(at, w)], db[i], d_sem.at[i]) for i, (at, w) in enumerate(dw)]

    for c in smalls:
        c.wait()
    abuf[...] = normed(xbuf[...].astype(F32), gab[...].astype(F32))
    cos, sin = rot[0, 0:1, :], rot[1, 0:1, :]
    for i, (at, w) in enumerate(qw):
        wqs[i].wait()
        q = jnp.dot(abuf[...], gb[i][:, 0:w], preferred_element_type=F32)
        for n in range(w // head):
            t = q[:, n * head : (n + 1) * head].astype(BF16).astype(F32)
            t = t * cos + pltpu.roll(t, head // 2, 1) * sin
            qbuf[pl.ds(at // head + n, batch, stride=heads), :] = t.astype(BF16).astype(F32)

    groups = batch // GROUP
    ring = SLOTS // GROUP
    shape = (heads, rows)
    own = lax.rem(lax.broadcasted_iota(jnp.int32, shape, 1), kv) == lax.div(lax.broadcasted_iota(jnp.int32, shape, 0), heads // kv)
    factor = math.log2(math.e) * head**-0.5

    def slot_of(g, i):
        return lax.rem(g, ring) * GROUP + i

    def scores_of(g, out):
        for i in range(GROUP):
            q = qbuf[pl.ds(pl.multiple_of((g * GROUP + i) * heads, heads), heads), :].astype(BF16)
            s = lax.dot_general(q, kbuf[slot_of(g, i)], (((1,), (1,)), ((), ())), preferred_element_type=F32)
            out[i] = s

    def seen_of(g, scores):
        for i in range(GROUP):
            s = jnp.where(own, scores[i], -jnp.inf)
            p = jnp.exp2((s - jnp.max(s, -1, keepdims=True)) * factor)
            p = (p * (1.0 / jnp.sum(p, -1, keepdims=True))).astype(BF16)
            o = jnp.dot(p, vbuf[slot_of(g, i)], preferred_element_type=F32)
            seen[pl.ds(pl.multiple_of((g * GROUP + i) * heads, heads), heads), :] = o.astype(BF16).astype(F32)

    def wait_k(g):
        for i in range(GROUP):
            k_copy(g * GROUP + i, slot_of(g, i)).wait()

    def wait_v(g):
        for i in range(GROUP):
            v_copy(g * GROUP + i, slot_of(g, i)).wait()

    def start_k(g):
        for i in range(GROUP):
            k_copy(g * GROUP + i, slot_of(g, i)).start()

    def start_v(g):
        for i in range(GROUP):
            v_copy(g * GROUP + i, slot_of(g, i)).start()

    wait_k(0)
    scores_of(0, sa)

    def step(g, now, later, last=False):
        if not last:
            wait_k(g + 1)
        wait_v(g)
        if not last:
            scores_of(g + 1, later)
        seen_of(g, now)

        if not last:

            @pl.when(g == 0)
            def _():
                start_k(ring)

            @pl.when(g + 1 + ring < groups)
            def _():
                start_k(g + 1 + ring)

            @pl.when(g + ring < groups)
            def _():
                start_v(g + ring)

            @pl.when(g + ring == groups)
            def _():
                for c in wos:
                    c.start()
                for c in [c for pair in zip(gs, us) for c in pair] + ds:
                    c.start()

    def two(i, carry):
        step(2 * i, sa, sb)
        step(2 * i + 1, sb, sa)
        return carry

    lax.fori_loop(0, groups // 2 - 1, two, 0)
    step(groups - 2, sa, sb)
    step(groups - 1, sb, sa, last=True)

    pl.semaphore_wait(barrier, 2)

    mine = pl.ds(pl.multiple_of(core * half, half), half)
    theirs = pl.ds(pl.multiple_of((1 - core) * half, half), half)

    def remote(src, dst, send, recv, to):
        return pltpu.make_async_remote_copy(src_ref=src, dst_ref=dst, send_sem=send, recv_sem=recv, device_id={"tp": to}, device_id_type=MESH)

    def summed(which, term, base, out):
        n = len(dw)
        one = [remote(sends1.at[which, c], recvs1.at[which, c], ss1.at[which, c], rs1.at[which, c], partner) for c in range(n)]
        two_ = [remote(sends2.at[which, c], recvs2.at[which, c], ss2.at[which, c], rs2.at[which, c], across) for c in range(n)]
        three = [remote(out.at[c, mine, :], out.at[c, mine, :], ss3.at[which, c], rs3.at[which, c], partner) for c in range(n)]
        for c in range(n):
            part[c] = term(c)
            sends1[which, c] = part[c, theirs, :].astype(BF16)
            one[c].start()
        for c in range(n):
            one[c].wait_recv()
            sends2[which, c] = (part[c, mine, :] + recvs1[which, c].astype(F32)).astype(BF16)
            two_[c].start()
        for c in range(n):
            two_[c].wait_recv()
            total = sends2[which, c].astype(F32) + recvs2[which, c].astype(F32)
            out[c, mine, :] = (base(c) + total).astype(BF16)
            three[c].start()
        for c in range(n):
            three[c].wait()
            one[c].wait_send()
            two_[c].wait_send()

    for n in range(heads):
        hidden[:, n * head : (n + 1) * head] = seen[pl.ds(n, batch, stride=heads), :].astype(BF16)

    def wo_term(c):
        wos[c].wait()
        return jnp.dot(hidden[:, 0:qcols], wob[c][...], preferred_element_type=F32)

    summed(0, wo_term, lambda c: xbuf[mine, pl.ds(dw[c][0], dw[c][1])].astype(F32), hbuf)

    squares = jnp.zeros((batch, 1), F32)
    for c in range(len(dw)):
        h = hbuf[c].astype(F32)
        squares = squares + jnp.sum(h * h, -1, keepdims=True)
    scale = lax.rsqrt(squares * (1.0 / d) + 1e-6)
    for c, (at, w) in enumerate(dw):
        bbuf[:, at : at + w] = (hbuf[c].astype(F32) * scale * gmb[:, at : at + w].astype(F32)).astype(BF16)

    for c, (at, w) in enumerate(ffw):
        gs[c].wait()
        us[c].wait()
        gate = jnp.dot(bbuf[...], gb[c][...], preferred_element_type=F32)
        up = jnp.dot(bbuf[...], ub[c][...], preferred_element_type=F32)
        hidden[:, at : at + w] = (gate * (1.0 / (1.0 + jnp.exp(-gate))) * up).astype(BF16)

    def down_term(c):
        ds[c].wait()
        return jnp.dot(hidden[...], db[c][...], preferred_element_type=F32)

    summed(1, down_term, lambda c: hbuf[c, mine, :].astype(F32), final)
    for c, (at, w) in enumerate(dw):
        y_ref[:, at : at + w] = final[c]


def solution(mesh):
    def step(x, k_cache, v_cache, gain_a, wq, wo, gain_m, w_gate, w_up, w_down):
        batch, cache, kv, head = k_cache.shape
        d, qcols = wq.shape
        heads, ff, rows = qcols // head, w_gate.shape[1], cache * kv
        dims = (batch, d, heads, kv, head, rows, ff)
        half = batch // 2
        ffw, dw = widths_of(ff, 512), widths_of(d, 512)
        n, w = len(dw), dw[0][1]
        dma = pltpu.SemaphoreType.DMA
        scratch = [
            pltpu.VMEM((SLOTS, rows, head), BF16),
            pltpu.VMEM((SLOTS, rows, head), BF16),
            pltpu.VMEM((batch, d), BF16),
            pltpu.VMEM((1, d), BF16),
            pltpu.VMEM((1, d), BF16),
            pltpu.VMEM((2, 8, head), F32),
            pltpu.VMEM((batch, d), BF16),
            pltpu.VMEM((batch * heads, head), F32),
            pltpu.VMEM((GROUP, heads, rows), F32),
            pltpu.VMEM((GROUP, heads, rows), F32),
            pltpu.VMEM((batch * heads, head), F32),
            pltpu.VMEM((n, batch, w), BF16),
            pltpu.VMEM((batch, d), BF16),
            pltpu.VMEM((batch, ff), BF16),
            pltpu.VMEM((n, batch, w), F32),
            *[pltpu.VMEM((qcols, w), BF16) for _, w in dw],
            *[pltpu.VMEM((d, w), BF16) for _, w in ffw],
            *[pltpu.VMEM((d, w), BF16) for _, w in ffw],
            *[pltpu.VMEM((ff, w), BF16) for _, w in dw],
            *[pltpu.VMEM((2, n, half, w), BF16) for _ in range(4)],
            pltpu.VMEM((n, batch, w), BF16),
            dma((4,)),
            dma((2,)),
            dma((SLOTS,)),
            dma((SLOTS,)),
            dma((n,)),
            dma((len(ffw),)),
            dma((len(ffw),)),
            dma((n,)),
            *[dma((2, n)) for _ in range(6)],
        ]
        hbm = pl.BlockSpec(memory_space=pltpu.HBM)
        return pl.pallas_call(
            functools.partial(layer, dims),
            out_shape=jax.ShapeDtypeStruct((batch, d), BF16),
            in_specs=[hbm] * 11,
            out_specs=pl.BlockSpec(memory_space=pltpu.VMEM),
            scratch_shapes=scratch,
            compiler_params=pltpu.CompilerParams(collective_id=0, has_side_effects=True, vmem_limit_bytes=67043328),
            name="decoder_layer",
        )(
            x,
            k_cache.reshape(batch, rows, head),
            v_cache.reshape(batch, rows, head),
            gain_a.reshape(1, d),
            wq,
            wo,
            gain_m.reshape(1, d),
            w_gate,
            w_up,
            w_down,
            rotary(head, cache - 1),
        )

    states, cache, columns, rows_of = P("dp", None), P("dp", None, "tp", None), P(None, "tp"), P("tp", None)
    return jax.shard_map(
        step,
        mesh=mesh,
        in_specs=(states, cache, cache, P(None), columns, rows_of, P(None), columns, columns, rows_of),
        out_specs=states,
        check_vma=False,
    )
```

time: 166 us -> 81.5 us (0.49)
  matrix products: 90 us -> 0 us
  Pallas kernels: 0 us -> 77 us
  waiting for transfers between devices: 56.7 us -> 0 us
  between operations: 13.5 us -> 0.01 us
  other arithmetic: 5 us -> 0 us
  local copies, waits for them, and re-layouts: 0.11 us -> 4.3 us
    pallas_call x0 -> x1, Pallas kernels: none -> 77 us  [step(): pl.pallas_call(functools.partial(layer, dims), out_shape=jax.ShapeDtypeSt...]
    psum x2 -> x0, waiting for transfers between devices: 56.6 us -> none  [added(): lax.psum(term.astype(jnp.bfloat16), 'tp').astype(jnp.float32)]
    dot_general x5 -> x0, matrix products: 54.6 us -> none  [the longest x1 26.6 us: einsum(): return jnp.einsum(form, a.astype(jnp.float32), b.astype(jnp.float32))]
    sub x1 -> x0, matrix products: 35.4 us -> none  [seen_by(): weights = jax.nn.softmax(scores, -1).astype(jnp.bfloat16)]
    reshape x1 -> x2, local copies, waits for them, and re-layouts: 0.07 us -> 2.59 us  [the longest x1 1.3 us: step(): gain_a.reshape(1, d)]
    convert_element_type x3 -> x0, other arithmetic: 2.48 us -> none  [the longest x1 1.77 us: added(): (t.astype(jnp.float32) + lax.psum(term.astype(jnp.bfloat16), 'tp').astype...]
    reduce_sum x2 -> x0, other arithmetic: 2.32 us -> none  [normed(): scale = lax.rsqrt(jnp.mean(wide * wide, -1, keepdims=True) + 1e-06)]
    unnamed x5 -> x1, local copies, waits for them, and re-layouts: 0.03 us -> 1.72 us
  transfers between devices with their start and end apart: 2 -> 0, of which waited for: 2 -> 0; matrix products, arithmetic and copies ran while one was open for 0% -> 0% of each run, Pallas kernels for 0% -> 0%
where the time goes in v1:
time: 81.5 us; the launch traced here: 81.3 us
  Pallas kernels  77 us (94%)
  local copies, waits for them, and re-layouts  4.3 us (5%)
    pallas_call x1, Pallas kernels, step(): pl.pallas_call(functools.partial(layer, dims), out_shape=jax.ShapeDtypeSt...  77 us
    unnamed x1, local copies, waits for them, and re-layouts  1.72 us

profile of v1, /device:TPU:0, one launch (start us, length us, event | category | flops | bytes accessed | tf_op | source)
XLA Modules:
  0.0 81.3 jit_solution(4866106496007658038)
XLA Ops:
  0.0 1.3 %reshape.14.ga_hbm = bf16[1,2560]{1,0:T(2,128)(2,1)} reshape(bf16[2560]{0:T(1024)(128)(2,1)} %param.14) | data formatting | bytes 10240 | tf_op jit(solution)/shard_map/reshape | solution.py:298
  1.3 1.3 %reshape.15.gm_hbm = bf16[1,2560]{1,0:T(2,128)(2,1)} reshape(bf16[2560]{0:T(1024)(128)(2,1)} %param.17) | data formatting | bytes 10240 | tf_op jit(solution)/shard_map/reshape | solution.py:301
  2.6 77.0 %decoder_layer.1 = bf16[64,2560]{1,0:T(8,128)(2,1)} custom-call(bf16[64,2560]{1,0:T(8,128)(2,1)} %x_hbm.1, bf16[64,4096,128]{2,1,0:T(8,128)(2,1)} %bitcast.k_hbm, bf16[64,4096,128]{2,1,0:T(8,128)(2,1)} %bitcast.1.v_hbm, bf16[1,2560]{1,0:T(2,128)(2,1)} %reshape.14.ga_hbm, bf16[2560,1024]{1,0:T(8,128)(2,1)} %wq_hbm.1, bf16[1024,2560]{1,0:T(8,128)(2,1)} %wo_hbm.1, ...), custom_call_target="tpu_custom_call" | custom-call | tf_op jit(solution)/shard_map/decoder_layer/pallas_call | solution.py:286
  79.6 1.7 %copy.13 = bf16[64,2560]{1,0:T(8,128)(2,1)} copy(bf16[64,2560]{1,0:T(8,128)(2,1)} %decoder_layer.1) | data formatting | bytes 655360

commit v2 on v1

--- a/solution.py
+++ b/solution.py
@@ -29,6 +29,11 @@
     return np.broadcast_to(rows[:, None], (2, 8, head)).astype(np.float32)
 
 
+def row_of(gain):
+    wide = gain[...].astype(F32)
+    return jnp.concatenate([wide[n : n + 1] for n in range(wide.shape[0])], -1)
+
+
 def normed(x, gain):
     scale = lax.rsqrt(jnp.mean(x * x, -1, keepdims=True) + 1e-6)
     return (x * scale * gain).astype(BF16)
@@ -86,7 +91,7 @@
 
     for c in smalls:
         c.wait()
-    abuf[...] = normed(xbuf[...].astype(F32), gab[...].astype(F32))
+    abuf[...] = normed(xbuf[...].astype(F32), row_of(gab))
     cos, sin = rot[0, 0:1, :], rot[1, 0:1, :]
     for i, (at, w) in enumerate(qw):
         wqs[i].wait()
@@ -165,7 +170,7 @@
                 for c in wos:
                     c.start()
                 for c in [c for pair in zip(gs, us) for c in pair] + ds:
-                    c.start()
+                    c.start(priority=1)
 
     def two(i, carry):
         step(2 * i, sa, sb)
@@ -221,8 +226,9 @@
         h = hbuf[c].astype(F32)
         squares = squares + jnp.sum(h * h, -1, keepdims=True)
     scale = lax.rsqrt(squares * (1.0 / d) + 1e-6)
+    gain = row_of(gmb)
     for c, (at, w) in enumerate(dw):
-        bbuf[:, at : at + w] = (hbuf[c].astype(F32) * scale * gmb[:, at : at + w].astype(F32)).astype(BF16)
+        bbuf[:, at : at + w] = (hbuf[c].astype(F32) * scale * gain[:, at : at + w]).astype(BF16)
 
     for c, (at, w) in enumerate(ffw):
         gs[c].wait()
@@ -254,8 +260,8 @@
             pltpu.VMEM((SLOTS, rows, head), BF16),
             pltpu.VMEM((SLOTS, rows, head), BF16),
             pltpu.VMEM((batch, d), BF16),
-            pltpu.VMEM((1, d), BF16),
-            pltpu.VMEM((1, d), BF16),
+            pltpu.VMEM((d // 128, 128), BF16),
+            pltpu.VMEM((d // 128, 128), BF16),
             pltpu.VMEM((2, 8, head), F32),
             pltpu.VMEM((batch, d), BF16),
             pltpu.VMEM((batch * heads, head), F32),
@@ -285,20 +291,20 @@
         hbm = pl.BlockSpec(memory_space=pltpu.HBM)
         return pl.pallas_call(
             functools.partial(layer, dims),
-            out_shape=jax.ShapeDtypeStruct((batch, d), BF16),
+            out_shape=pltpu.VMEM((batch, d), BF16),
             in_specs=[hbm] * 11,
             out_specs=pl.BlockSpec(memory_space=pltpu.VMEM),
             scratch_shapes=scratch,
-            compiler_params=pltpu.CompilerParams(collective_id=0, has_side_effects=True, vmem_limit_bytes=67043328),
+            compiler_params=pltpu.CompilerParams(collective_id=0, has_side_effects=True, vmem_limit_bytes=66000000),
             name="decoder_layer",
         )(
             x,
             k_cache.reshape(batch, rows, head),
             v_cache.reshape(batch, rows, head),
-            gain_a.reshape(1, d),
+            gain_a.reshape(d // 128, 128),
             wq,
             wo,
-            gain_m.reshape(1, d),
+            gain_m.reshape(d // 128, 128),
             w_gate,
             w_up,
             w_down,

time: 81.5 us -> 69.4 us (0.85)
  Pallas kernels: 77 us -> 68.5 us
  local copies, waits for them, and re-layouts: 4.3 us -> 0.73 us
    pallas_call x1, Pallas kernels: 77 us -> 68.5 us  [step(): pl.pallas_call(functools.partial(layer, dims), out_shape=pltpu.VMEM((batc...]
    reshape x2 -> x0, local copies, waits for them, and re-layouts: 2.59 us -> none  [the longest x1 1.3 us: step(): gain_a.reshape(1, d)]
    unnamed x1, local copies, waits for them, and re-layouts: 1.72 us -> 0.73 us
where the time goes in v2:
time: 69.4 us; the launch traced here: 69.3 us
  Pallas kernels  68.5 us (99%)
  local copies, waits for them, and re-layouts  0.73 us (1%)
    pallas_call x1, Pallas kernels, step(): pl.pallas_call(functools.partial(layer, dims), out_shape=pltpu.VMEM((batc...  68.5 us

profile of v2, /device:TPU:0, one launch (start us, length us, event | category | flops | bytes accessed | tf_op | source)
XLA Modules:
  0.0 69.3 jit_solution(658936553879562513)
XLA Ops:
  0.0 68.5 %decoder_layer.1 = bf16[64,2560]{1,0:T(8,128)(2,1)S(1)} custom-call(bf16[64,2560]{1,0:T(8,128)(2,1)} %x_hbm.1, bf16[64,4096,128]{2,1,0:T(8,128)(2,1)} %bitcast.k_hbm, bf16[64,4096,128]{2,1,0:T(8,128)(2,1)} %bitcast.1.v_hbm, bf16[20,128]{1,0:T(8,128)(2,1)} %bitcast.4, bf16[2560,1024]{1,0:T(8,128)(2,1)} %wq_hbm.1, bf16[1024,2560]{1,0:T(8,128)(2,1)} %wo_hbm.1, ...), custom_call_target="tpu_custom_call" | custom-call | tf_op jit(solution)/shard_map/decoder_layer/pallas_call | solution.py:292
  68.5 0.7 %copy.13 = bf16[64,2560]{1,0:T(8,128)(2,1)} copy(bf16[64,2560]{1,0:T(8,128)(2,1)S(1)} %decoder_layer.1) | data formatting | bytes 655360

commit v3 on v2

v3 whole, which is shorter than its diff:
```python
import functools
import math

import jax
import jax.numpy as jnp
import numpy as np
from jax import lax
from jax.experimental import pallas as pl
from jax.experimental.pallas import tpu as pltpu
from jax.sharding import PartitionSpec as P

THETA = 10000
MESH = pl.DeviceIdType.MESH
F32, BF16 = jnp.float32, jnp.bfloat16

GROUP = 2
SLOTS = 8
LAG = 2
BLOCK = 8


def widths_of(total, width):
    return [(at, min(width, total - at)) for at in range(0, total, width)]


def rotary(head, place):
    half = head // 2
    angle = place * float(THETA) ** (-np.arange(half, dtype=np.float64) / half)
    cos, sin = np.cos(angle), np.sin(angle)
    rows = np.stack([np.concatenate([cos, cos]), np.concatenate([-sin, sin])])
    return np.broadcast_to(rows[:, None], (2, 8, head)).astype(np.float32)


def row_of(gain):
    wide = gain[...].astype(F32)
    return jnp.concatenate([wide[n : n + 1] for n in range(wide.shape[0])], -1)


def normed(x, gain):
    scale = lax.rsqrt(jnp.mean(x * x, -1, keepdims=True) + 1e-6)
    return (x * scale * gain).astype(BF16)


def layer(dims, x_hbm, k_hbm, v_hbm, ga_hbm, wq_hbm, wo_hbm, gm_hbm, wg_hbm, wu_hbm, wd_hbm, rot_hbm, y_ref, *scratch):
    batch, d, heads, kv, head, rows, ff = dims
    qcols = heads * head
    half = batch // 2
    ffw, dw, qw, ow = widths_of(ff, 512), widths_of(d, 512), widths_of(qcols, 512), widths_of(d, d // 2)
    it = iter(scratch)

    def take(n):
        return [next(it) for _ in range(n)]

    (kbuf, vbuf, xbuf, gab, gmb, rot, bbuf, qbuf, sa, sb, seen, states, wide, hidden) = take(14)
    wob = take(len(ow))
    gb, ub = take(len(ffw)), take(len(ffw))
    db = take(len(dw))
    terms, others, sends1, recvs1, sends2, recvs2 = take(6)
    (small_sem, wq_sem, k_sem, v_sem, wo_sem, g_sem, u_sem, d_sem, ts, tr, ss1, rs1, ss2, rs2, ss3, rs3) = take(16)

    tp = lax.axis_index("tp")
    core = lax.rem(tp, 2)
    chip = lax.div(tp, 2)
    partner = chip * 2 + 1 - core
    across = (1 - chip) * 2 + core
    diagonal = (1 - chip) * 2 + 1 - core
    peers = (partner, across, diagonal)

    barrier = pltpu.get_barrier_semaphore()
    for other in peers:
        pl.semaphore_signal(barrier, inc=1, device_id={"tp": other}, device_id_type=MESH)

    copy = pltpu.make_async_copy
    smalls = [copy(x_hbm, xbuf, small_sem.at[0]), copy(ga_hbm, gab, small_sem.at[1]), copy(gm_hbm, gmb, small_sem.at[2]), copy(rot_hbm, rot, small_sem.at[3])]
    for c in smalls:
        c.start()
    wqs = [copy(wq_hbm.at[:, pl.ds(at, w)], gb[i].at[:, pl.ds(0, w)], wq_sem.at[i]) for i, (at, w) in enumerate(qw)]
    for c in wqs:
        c.start()

    def k_copy(seq, slot):
        return copy(k_hbm.at[seq], kbuf.at[slot], k_sem.at[slot])

    def v_copy(seq, slot):
        return copy(v_hbm.at[seq], vbuf.at[slot], v_sem.at[slot])

    for s in range(SLOTS):
        k_copy(s, s).start()
        v_copy(s, s).start()

    wos = [copy(wo_hbm.at[:, pl.ds(at, w)], wob[i], wo_sem.at[i]) for i, (at, w) in enumerate(ow)]
    gs = [copy(wg_hbm.at[:, pl.ds(at, w)], gb[i], g_sem.at[i]) for i, (at, w) in enumerate(ffw)]
    us = [copy(wu_hbm.at[:, pl.ds(at, w)], ub[i], u_sem.at[i]) for i, (at, w) in enumerate(ffw)]
    ds = [copy(wd_hbm.at[:, pl.ds(at, w)], db[i], d_sem.at[i]) for i, (at, w) in enumerate(dw)]
    for c in wos:
        c.start()

    for c in smalls:
        c.wait()
    states[...] = xbuf[...].astype(F32)
    bbuf[...] = normed(states[...], row_of(gab)).astype(BF16)
    cos, sin = rot[0, 0:1, :], rot[1, 0:1, :]
    for i, (at, w) in enumerate(qw):
        wqs[i].wait()
        q = jnp.dot(bbuf[...], gb[i][:, 0:w], preferred_element_type=F32)
        for n in range(w // head):
            t = q[:, n * head : (n + 1) * head].astype(BF16).astype(F32)
            t = t * cos + pltpu.roll(t, head // 2, 1) * sin
            qbuf[pl.ds(at // head + n, batch, stride=heads), :] = t.astype(BF16).astype(F32)

    groups = batch // GROUP
    ring = SLOTS // GROUP
    shape = (heads, rows)
    own = lax.rem(lax.broadcasted_iota(jnp.int32, shape, 1), kv) == lax.div(lax.broadcasted_iota(jnp.int32, shape, 0), heads // kv)
    factor = math.log2(math.e) * head**-0.5

    def slot_of(g, i):
        return lax.rem(g, ring) * GROUP + i

    def rows_of(g, i):
        return pl.ds(pl.multiple_of((g * GROUP + i) * heads, heads), heads)

    def scores_of(g, out):
        for i in range(GROUP):
            q = qbuf[rows_of(g, i), :].astype(BF16)
            out[i] = lax.dot_general(q, kbuf[slot_of(g, i)], (((1,), (1,)), ((), ())), preferred_element_type=F32)

    def weights_of(scores, i):
        s = jnp.where(own, scores[i], -jnp.inf)
        p = jnp.exp2((s - jnp.max(s, -1, keepdims=True)) * factor)
        return (p * (1.0 / jnp.sum(p, -1, keepdims=True))).astype(BF16)

    def seen_of(g, i, p):
        o = jnp.dot(p, vbuf[slot_of(g, i)], preferred_element_type=F32)
        seen[rows_of(g, i), :] = o.astype(BF16).astype(F32)

    def wait_k(g):
        for i in range(GROUP):
            k_copy(g * GROUP + i, slot_of(g, i)).wait()

    def wait_v(g, i):
        v_copy(g * GROUP + i, slot_of(g, i)).wait()

    def start_k(g):
        for i in range(GROUP):
            k_copy(g * GROUP + i, slot_of(g, i)).start()

    def start_v(g):
        for i in range(GROUP):
            v_copy(g * GROUP + i, slot_of(g, i)).start()

    def step(g, now, later):
        wait_k(g + 1)
        for i in range(GROUP):
            wait_v(g, i)
        scores_of(g + 1, later)
        for i in range(GROUP):
            seen_of(g, i, weights_of(now, i))

        @pl.when(g + 1 + ring < groups)
        def _():
            start_k(g + 1 + ring)

        @pl.when(g + ring < groups)
        def _():
            start_v(g + ring)

        @pl.when(g + ring == groups)
        def _():
            for c in [c for pair in zip(gs, us) for c in pair]:
                c.start(priority=1)

    def tail(g, now, later):
        wait_k(g + 1)
        scores_of(g + 1, later)
        ps = [weights_of(scores, i) for scores in (now, later) for i in range(GROUP)]
        for m in range(2):
            for i in range(GROUP):
                wait_v(g + m, i)
                seen_of(g + m, i, ps[m * GROUP + i])

    def remote(src, dst, send, recv, to):
        return pltpu.make_async_remote_copy(src_ref=src, dst_ref=dst, send_sem=send, recv_sem=recv, device_id={"tp": to}, device_id_type=MESH)

    def exchanges(b, n, c):
        at = pl.ds(b, n)
        return [remote(terms.at[c, at], others.at[p, c, at], ts.at[p, c, b], tr.at[p, c, b], to) for p, to in enumerate(peers)]

    def send_terms(b, n):
        rows = n * BLOCK
        block = [seen[pl.ds(b * (BLOCK * heads) + m, rows, stride=heads), :] for m in range(heads)]
        block = jnp.concatenate(block, -1).astype(BF16)
        for c, (at, w) in enumerate(ow):
            term = jnp.dot(block, wob[c][...], preferred_element_type=F32)
            terms[c, pl.ds(b, n)] = term.reshape(n, BLOCK, w).astype(BF16)
            for e in exchanges(b, n, c):
                e.start()

    def add_terms(b, n):
        rows = n * BLOCK
        at_rows = pl.ds(b * BLOCK, rows)
        squares = jnp.zeros((rows, 1), F32)
        for c, (at, w) in enumerate(ow):
            for e in exchanges(b, n, c):
                e.wait()
            t = [terms[c, pl.ds(b, n)]] + [others[p, c, pl.ds(b, n)] for p in range(3)]
            t = [v.astype(F32).reshape(rows, w) for v in t]
            h = states[at_rows, at : at + w] + ((t[0] + t[1]) + (t[2] + t[3]))
            h = h.astype(BF16).astype(F32)
            states[at_rows, at : at + w] = h
            squares = squares + jnp.sum(h * h, -1, keepdims=True)
        scale = lax.rsqrt(squares * (1.0 / d) + 1e-6)
        wide[at_rows, :] = states[at_rows, :] * scale * row_of(gmb)

    wait_k(0)
    scores_of(0, sa)
    start_k(ring)
    for c in wos:
        c.wait()
    pl.semaphore_wait(barrier, 3)
    trips, blocks = groups // 2, batch // BLOCK
    ahead = 2 * BLOCK // (2 * GROUP)
    early = blocks - 2

    def two(i, carry):
        step(2 * i, sa, sb)
        step(2 * i + 1, sb, sa)

        @pl.when(jnp.logical_and(lax.rem(i, ahead) == ahead - 1, i < trips - ahead))
        def _():
            send_terms(lax.div(i, ahead) * 2, 2)

        @pl.when(i == trips - 1 - ahead // 2)
        def _():
            send_terms(early, 1)

        return carry

    lax.fori_loop(0, trips - 1, two, 0)
    tail(groups - 2, sa, sb)
    send_terms(blocks - 1, 1)
    for c in ds:
        c.start(priority=1)
    for b in range(0, early, 2):
        add_terms(b, 2)
    add_terms(early, 1)
    add_terms(early + 1, 1)
    bbuf[...] = wide[...].astype(BF16)

    for c, (at, w) in enumerate(ffw):
        gs[c].wait()
        us[c].wait()
        gate = jnp.dot(bbuf[...], gb[c][...], preferred_element_type=F32)
        up = jnp.dot(bbuf[...], ub[c][...], preferred_element_type=F32)
        hidden[:, at : at + w] = (gate * (1.0 / (1.0 + jnp.exp(-gate))) * up).astype(BF16)

    which = lax.rem(core + chip, 2)
    mine = pl.ds(pl.multiple_of(which * half, half), half)
    theirs = pl.ds(pl.multiple_of((1 - which) * half, half), half)
    n = len(dw)
    one = [remote(sends1.at[c], recvs1.at[c], ss1.at[c], rs1.at[c], partner) for c in range(n)]
    two = [remote(sends2.at[c], recvs2.at[c], ss2.at[c], rs2.at[c], diagonal) for c in range(n)]
    spots = [y_ref.at[mine, pl.ds(at, w)] for at, w in dw]
    three = [remote(spots[c], spots[c], ss3.at[c], rs3.at[c], partner) for c in range(n)]

    def send_half(c):
        at, w = dw[c]
        wide[:, at : at + w] = jnp.dot(hidden[...], db[c][...], preferred_element_type=F32)
        sends1[c] = wide[theirs, at : at + w].astype(BF16)
        one[c].start()

    def send_chip(c):
        at, w = dw[c]
        one[c].wait_recv()
        sends2[c] = (wide[mine, at : at + w] + recvs1[c].astype(F32)).astype(BF16)
        two[c].start()

    def finish(c):
        at, w = dw[c]
        two[c].wait_recv()
        y_ref[mine, at : at + w] = (states[mine, at : at + w] + (sends2[c].astype(F32) + recvs2[c].astype(F32))).astype(BF16)
        three[c].start()

    for c in range(n + LAG):
        if c < n:
            ds[c].wait()
            send_half(c)
        if c >= LAG:
            send_chip(c - LAG)
    for c in range(n):
        finish(c)
    for c in range(n):
        three[c].wait()
        one[c].wait_send()
        two[c].wait_send()


def solution(mesh):
    def step(x, k_cache, v_cache, gain_a, wq, wo, gain_m, w_gate, w_up, w_down):
        batch, cache, kv, head = k_cache.shape
        d, qcols = wq.shape
        heads, ff, rows = qcols // head, w_gate.shape[1], cache * kv
        dims = (batch, d, heads, kv, head, rows, ff)
        half = batch // 2
        ffw, dw, ow = widths_of(ff, 512), widths_of(d, 512), widths_of(d, d // 2)
        n, w, blocks = len(dw), dw[0][1], batch // BLOCK
        dma = pltpu.SemaphoreType.DMA
        scratch = [
            pltpu.VMEM((SLOTS, rows, head), BF16),
            pltpu.VMEM((SLOTS, rows, head), BF16),
            pltpu.VMEM((batch, d), BF16),
            pltpu.VMEM((d // 128, 128), BF16),
            pltpu.VMEM((d // 128, 128), BF16),
            pltpu.VMEM((2, 8, head), F32),
            pltpu.VMEM((batch, d), BF16),
            pltpu.VMEM((batch * heads, head), F32),
            pltpu.VMEM((GROUP, heads, rows), F32),
            pltpu.VMEM((GROUP, heads, rows), F32),
            pltpu.VMEM((batch * heads, head), F32),
            pltpu.VMEM((batch, d), F32),
            pltpu.VMEM((batch, d), F32),
            pltpu.VMEM((batch, ff), BF16),
            *[pltpu.VMEM((qcols, w), BF16) for _, w in ow],
            *[pltpu.VMEM((d, w), BF16) for _, w in ffw],
            *[pltpu.VMEM((d, w), BF16) for _, w in ffw],
            *[pltpu.VMEM((ff, w), BF16) for _, w in dw],
            pltpu.VMEM((2, blocks, BLOCK, d // 2), BF16),
            pltpu.VMEM((3, 2, blocks, BLOCK, d // 2), BF16),
            *[pltpu.VMEM((n, half, w), BF16) for _ in range(4)],
            dma((4,)),
            dma((2,)),
            dma((SLOTS,)),
            dma((SLOTS,)),
            dma((2,)),
            dma((len(ffw),)),
            dma((len(ffw),)),
            dma((n,)),
            dma((3, 2, blocks)),
            dma((3, 2, blocks)),
            *[dma((n,)) for _ in range(6)],
        ]
        hbm = pl.BlockSpec(memory_space=pltpu.HBM)
        return pl.pallas_call(
            functools.partial(layer, dims),
            out_shape=pltpu.VMEM((batch, d), BF16),
            in_specs=[hbm] * 11,
            out_specs=pl.BlockSpec(memory_space=pltpu.VMEM),
            scratch_shapes=scratch,
            compiler_params=pltpu.CompilerParams(collective_id=0, has_side_effects=True, vmem_limit_bytes=66000000),
            name="decoder_layer",
        )(
            x,
            k_cache.reshape(batch, rows, head),
            v_cache.reshape(batch, rows, head),
            gain_a.reshape(d // 128, 128),
            wq,
            wo,
            gain_m.reshape(d // 128, 128),
            w_gate,
            w_up,
            w_down,
            rotary(head, cache - 1),
        )

    states, cache, columns, rows_of = P("dp", None), P("dp", None, "tp", None), P(None, "tp"), P("tp", None)
    return jax.shard_map(
        step,
        mesh=mesh,
        in_specs=(states, cache, cache, P(None), columns, rows_of, P(None), columns, columns, rows_of),
        out_specs=states,
        check_vma=False,
    )
```

time: 69.4 us -> 65.7 us (0.947)
  Pallas kernels: 68.5 us -> 64.8 us
    pallas_call x1, Pallas kernels: 68.5 us -> 64.8 us  [step(): pl.pallas_call(functools.partial(layer, dims), out_shape=pltpu.VMEM((batc...]
where the time goes in v3:
time: 65.7 us; the launch traced here: 65.6 us
  Pallas kernels  64.8 us (99%)
  local copies, waits for them, and re-layouts  0.73 us (1%)
    pallas_call x1, Pallas kernels, step(): pl.pallas_call(functools.partial(layer, dims), out_shape=pltpu.VMEM((batc...  64.8 us

profile of v3, /device:TPU:0, one launch (start us, length us, event | category | flops | bytes accessed | tf_op | source)
XLA Modules:
  0.0 65.6 jit_solution(8823753129108526439)
XLA Ops:
  0.0 64.8 %decoder_layer.1 = bf16[64,2560]{1,0:T(8,128)(2,1)S(1)} custom-call(bf16[64,2560]{1,0:T(8,128)(2,1)} %x_hbm.1, bf16[64,4096,128]{2,1,0:T(8,128)(2,1)} %bitcast.k_hbm, bf16[64,4096,128]{2,1,0:T(8,128)(2,1)} %bitcast.1.v_hbm, bf16[20,128]{1,0:T(8,128)(2,1)} %bitcast.4, bf16[2560,1024]{1,0:T(8,128)(2,1)} %wq_hbm.1, bf16[1024,2560]{1,0:T(8,128)(2,1)} %wo_hbm.1, ...), custom_call_target="tpu_custom_call" | custom-call | tf_op jit(solution)/shard_map/decoder_layer/pallas_call | solution.py:343
  64.9 0.7 %copy.13 = bf16[64,2560]{1,0:T(8,128)(2,1)} copy(bf16[64,2560]{1,0:T(8,128)(2,1)S(1)} %decoder_layer.1) | data formatting | bytes 655360

commit v4 on v3

--- a/solution.py
+++ b/solution.py
@@ -16,6 +16,7 @@
 GROUP = 2
 SLOTS = 8
 LAG = 2
+FIRST = 4
 BLOCK = 8
 
 
@@ -84,7 +85,7 @@
     def v_copy(seq, slot):
         return copy(v_hbm.at[seq], vbuf.at[slot], v_sem.at[slot])
 
-    for s in range(SLOTS):
+    for s in range(FIRST):
         k_copy(s, s).start()
         v_copy(s, s).start()
 
@@ -92,8 +93,6 @@
     gs = [copy(wg_hbm.at[:, pl.ds(at, w)], gb[i], g_sem.at[i]) for i, (at, w) in enumerate(ffw)]
     us = [copy(wu_hbm.at[:, pl.ds(at, w)], ub[i], u_sem.at[i]) for i, (at, w) in enumerate(ffw)]
     ds = [copy(wd_hbm.at[:, pl.ds(at, w)], db[i], d_sem.at[i]) for i, (at, w) in enumerate(dw)]
-    for c in wos:
-        c.start()
 
     for c in smalls:
         c.wait()
@@ -102,6 +101,10 @@
     cos, sin = rot[0, 0:1, :], rot[1, 0:1, :]
     for i, (at, w) in enumerate(qw):
         wqs[i].wait()
+        if i == 0:
+            for s in range(FIRST, SLOTS):
+                k_copy(s, s).start()
+                v_copy(s, s).start()
         q = jnp.dot(bbuf[...], gb[i][:, 0:w], preferred_element_type=F32)
         for n in range(w // head):
             t = q[:, n * head : (n + 1) * head].astype(BF16).astype(F32)
@@ -216,7 +219,7 @@
     scores_of(0, sa)
     start_k(ring)
     for c in wos:
-        c.wait()
+        c.start()
     pl.semaphore_wait(barrier, 3)
     trips, blocks = groups // 2, batch // BLOCK
     ahead = 2 * BLOCK // (2 * GROUP)
@@ -225,6 +228,11 @@
     def two(i, carry):
         step(2 * i, sa, sb)
         step(2 * i + 1, sb, sa)
+
+        @pl.when(i == ahead - 1)
+        def _():
+            for c in wos:
+                c.wait()
 
         @pl.when(jnp.logical_and(lax.rem(i, ahead) == ahead - 1, i < trips - ahead))
         def _():

time: 65.7 us -> 64.5 us (0.982)
  Pallas kernels: 64.8 us -> 63.7 us
    pallas_call x1, Pallas kernels: 64.8 us -> 63.7 us  [step(): pl.pallas_call(functools.partial(layer, dims), out_shape=pltpu.VMEM((batc...]
where the time goes in v4:
time: 64.5 us; the launch traced here: 64.4 us
  Pallas kernels  63.7 us (99%)
  local copies, waits for them, and re-layouts  0.73 us (1%)
    pallas_call x1, Pallas kernels, step(): pl.pallas_call(functools.partial(layer, dims), out_shape=pltpu.VMEM((batc...  63.7 us

profile of v4, /device:TPU:0, one launch (start us, length us, event | category | flops | bytes accessed | tf_op | source)
XLA Modules:
  0.0 64.4 jit_solution(14553557901066671049)
XLA Ops:
  0.0 63.7 %decoder_layer.1 = bf16[64,2560]{1,0:T(8,128)(2,1)S(1)} custom-call(bf16[64,2560]{1,0:T(8,128)(2,1)} %x_hbm.1, bf16[64,4096,128]{2,1,0:T(8,128)(2,1)} %bitcast.k_hbm, bf16[64,4096,128]{2,1,0:T(8,128)(2,1)} %bitcast.1.v_hbm, bf16[20,128]{1,0:T(8,128)(2,1)} %bitcast.4, bf16[2560,1024]{1,0:T(8,128)(2,1)} %wq_hbm.1, bf16[1024,2560]{1,0:T(8,128)(2,1)} %wo_hbm.1, ...), custom_call_target="tpu_custom_call" | custom-call | tf_op jit(solution)/shard_map/decoder_layer/pallas_call | solution.py:351
  63.7 0.7 %copy.13 = bf16[64,2560]{1,0:T(8,128)(2,1)} copy(bf16[64,2560]{1,0:T(8,128)(2,1)S(1)} %decoder_layer.1) | data formatting | bytes 655360

commit v5 on v4

--- a/solution.py
+++ b/solution.py
@@ -46,7 +46,7 @@
     batch, d, heads, kv, head, rows, ff = dims
     qcols = heads * head
     half = batch // 2
-    ffw, dw, qw, ow = widths_of(ff, 512), widths_of(d, 512), widths_of(qcols, 512), widths_of(d, d // 2)
+    ffw, dw, qw, ow = widths_of(ff, 1024), widths_of(d, 512), widths_of(qcols, 512), widths_of(d, d)
     it = iter(scratch)
 
     def take(n):
@@ -310,7 +310,7 @@
         heads, ff, rows = qcols // head, w_gate.shape[1], cache * kv
         dims = (batch, d, heads, kv, head, rows, ff)
         half = batch // 2
-        ffw, dw, ow = widths_of(ff, 512), widths_of(d, 512), widths_of(d, d // 2)
+        ffw, dw, ow = widths_of(ff, 1024), widths_of(d, 512), widths_of(d, d)
         n, w, blocks = len(dw), dw[0][1], batch // BLOCK
         dma = pltpu.SemaphoreType.DMA
         scratch = [
@@ -332,8 +332,8 @@
             *[pltpu.VMEM((d, w), BF16) for _, w in ffw],
             *[pltpu.VMEM((d, w), BF16) for _, w in ffw],
             *[pltpu.VMEM((ff, w), BF16) for _, w in dw],
-            pltpu.VMEM((2, blocks, BLOCK, d // 2), BF16),
-            pltpu.VMEM((3, 2, blocks, BLOCK, d // 2), BF16),
+            pltpu.VMEM((1, blocks, BLOCK, d), BF16),
+            pltpu.VMEM((3, 1, blocks, BLOCK, d), BF16),
             *[pltpu.VMEM((n, half, w), BF16) for _ in range(4)],
             dma((4,)),
             dma((2,)),
@@ -343,8 +343,8 @@
             dma((len(ffw),)),
             dma((len(ffw),)),
             dma((n,)),
-            dma((3, 2, blocks)),
-            dma((3, 2, blocks)),
+            dma((3, 1, blocks)),
+            dma((3, 1, blocks)),
             *[dma((n,)) for _ in range(6)],
         ]
         hbm = pl.BlockSpec(memory_space=pltpu.HBM)

time: 64.5 us -> 63.7 us (0.988)
  Pallas kernels: 63.7 us -> 62.9 us
    pallas_call x1, Pallas kernels: 63.7 us -> 62.9 us  [step(): pl.pallas_call(functools.partial(layer, dims), out_shape=pltpu.VMEM((batc...]
where the time goes in v5:
time: 63.7 us; the launch traced here: 63.6 us
  Pallas kernels  62.9 us (99%)
  local copies, waits for them, and re-layouts  0.73 us (1%)
    pallas_call x1, Pallas kernels, step(): pl.pallas_call(functools.partial(layer, dims), out_shape=pltpu.VMEM((batc...  62.9 us

profile of v5, /device:TPU:0, one launch (start us, length us, event | category | flops | bytes accessed | tf_op | source)
XLA Modules:
  0.0 63.6 jit_solution(9073692917547795490)
XLA Ops:
  0.0 62.9 %decoder_layer.1 = bf16[64,2560]{1,0:T(8,128)(2,1)S(1)} custom-call(bf16[64,2560]{1,0:T(8,128)(2,1)} %x_hbm.1, bf16[64,4096,128]{2,1,0:T(8,128)(2,1)} %bitcast.k_hbm, bf16[64,4096,128]{2,1,0:T(8,128)(2,1)} %bitcast.1.v_hbm, bf16[20,128]{1,0:T(8,128)(2,1)} %bitcast.4, bf16[2560,1024]{1,0:T(8,128)(2,1)} %wq_hbm.1, bf16[1024,2560]{1,0:T(8,128)(2,1)} %wo_hbm.1, ...), custom_call_target="tpu_custom_call" | custom-call | tf_op jit(solution)/shard_map/decoder_layer/pallas_call | solution.py:351
  62.9 0.7 %copy.13 = bf16[64,2560]{1,0:T(8,128)(2,1)} copy(bf16[64,2560]{1,0:T(8,128)(2,1)S(1)} %decoder_layer.1) | data formatting | bytes 655360

commit v6 on v5

--- a/solution.py
+++ b/solution.py
@@ -222,25 +222,22 @@
         c.start()
     pl.semaphore_wait(barrier, 3)
     trips, blocks = groups // 2, batch // BLOCK
-    ahead = 2 * BLOCK // (2 * GROUP)
-    early = blocks - 2
+    each = BLOCK // (2 * GROUP)
+    first = 3 if blocks % 2 == 0 else 2
 
     def two(i, carry):
         step(2 * i, sa, sb)
         step(2 * i + 1, sb, sa)
 
-        @pl.when(i == ahead - 1)
+        @pl.when(i == first * each - 1)
         def _():
             for c in wos:
                 c.wait()
-
-        @pl.when(jnp.logical_and(lax.rem(i, ahead) == ahead - 1, i < trips - ahead))
-        def _():
-            send_terms(lax.div(i, ahead) * 2, 2)
-
-        @pl.when(i == trips - 1 - ahead // 2)
-        def _():
-            send_terms(early, 1)
+            send_terms(0, first)
+
+        @pl.when(jnp.logical_and(i >= first * each, lax.rem(i - first * each, 2 * each) == 2 * each - 1))
+        def _():
+            send_terms(lax.div(i + 1, each) - 2, 2)
 
         return carry
 
@@ -249,10 +246,10 @@
     send_terms(blocks - 1, 1)
     for c in ds:
         c.start(priority=1)
-    for b in range(0, early, 2):
+    add_terms(0, first)
+    for b in range(first, blocks - 1, 2):
         add_terms(b, 2)
-    add_terms(early, 1)
-    add_terms(early + 1, 1)
+    add_terms(blocks - 1, 1)
     bbuf[...] = wide[...].astype(BF16)
 
     for c, (at, w) in enumerate(ffw):

time: 63.7 us -> 63.7 us (level)
  no operation moved by 1% of the time
where the time goes in v6:
time: 63.7 us; the launch traced here: 63.6 us
  Pallas kernels  62.9 us (99%)
  local copies, waits for them, and re-layouts  0.73 us (1%)
    pallas_call x1, Pallas kernels, step(): pl.pallas_call(functools.partial(layer, dims), out_shape=pltpu.VMEM((batc...  62.9 us

profile of v6, /device:TPU:0, one launch (start us, length us, event | category | flops | bytes accessed | tf_op | source)
XLA Modules:
  0.0 63.6 jit_solution(16341103606817698701)
XLA Ops:
  0.0 62.9 %decoder_layer.1 = bf16[64,2560]{1,0:T(8,128)(2,1)S(1)} custom-call(bf16[64,2560]{1,0:T(8,128)(2,1)} %x_hbm.1, bf16[64,4096,128]{2,1,0:T(8,128)(2,1)} %bitcast.k_hbm, bf16[64,4096,128]{2,1,0:T(8,128)(2,1)} %bitcast.1.v_hbm, bf16[20,128]{1,0:T(8,128)(2,1)} %bitcast.4, bf16[2560,1024]{1,0:T(8,128)(2,1)} %wq_hbm.1, bf16[1024,2560]{1,0:T(8,128)(2,1)} %wo_hbm.1, ...), custom_call_target="tpu_custom_call" | custom-call | tf_op jit(solution)/shard_map/decoder_layer/pallas_call | solution.py:348
  62.9 0.7 %copy.13 = bf16[64,2560]{1,0:T(8,128)(2,1)} copy(bf16[64,2560]{1,0:T(8,128)(2,1)S(1)} %decoder_layer.1) | data formatting | bytes 655360
